TPU v7x, 32 devices: a whole 2x2x4 slice. The times are simulated.
32 devices in a mesh: pix: 8 (over y, x, core), row: 4 (over z).
Axes of the slice: x: 2, y: 2, z: 4, core: 2. Of those that a mesh axis runs over, the one named last changes fastest.
Arguments:
- band_images: bfloat16 [256, 128, 512], P('pix', 'row'), may hold values from -6 to 6
- pivots: int32 [2, 32], replicated, may hold values from 0 to 65535, as said below
Outputs:
- residual: bfloat16 [512, 128, 256], P(('pix', 'row'))
- coefficients: bfloat16 [64, 512, 128], P(None, ('pix', 'row'))
Inputs may be any that keep to these rules, and one draw needn't show every extreme that they name: All 64 pivots lie in different columns, and every group of 32 lines starting at a multiple of 32 holds at least one pivot.
All inputs are finite; a program needn't handle non-finite values.
Results may differ from a plain program's by a relative error of at most 0.001.
Values may be sent and summed in bfloat16 or wider, within the bound.
No kernel may reach another device: no remote copies, remote signals or barrier semaphores. Data moves between devices by JAX's collectives and lax.ppermute only.
A program may use at most 192 MiB of HBM per device.

v0:
```python
import jax
import jax.numpy as jnp
from jax import lax
from jax.sharding import PartitionSpec as P

highest = lax.Precision.HIGHEST


def orthonormal(spectra):
    gram = jnp.dot(spectra, spectra.T, precision=highest)
    factor = jnp.linalg.cholesky(gram)
    return jax.scipy.linalg.solve_triangular(factor, spectra, lower=True)


def project(block, basis):
    count = basis.shape[0] // 2
    first = basis[:count]
    second = basis[count:]
    coef_one = jnp.einsum("clb,kb->kcl", block, first, precision=highest)
    remain = block - jnp.einsum("kcl,kb->clb", coef_one, first, precision=highest)
    coef_two = jnp.einsum("clb,kb->kcl", remain, second, precision=highest)
    remain = remain - jnp.einsum("kcl,kb->clb", coef_two, second, precision=highest)
    return (
        remain.astype(jnp.bfloat16),
        jnp.concatenate([coef_one, coef_two], axis=0).astype(jnp.bfloat16),
    )


def shards(band_images, pivots):
    band_dev, line_dev, cols_all = band_images.shape
    pix_count = lax.axis_size("pix")
    row_count = lax.axis_size("row")
    narrow = cols_all // (pix_count * row_count)
    flat_pivots = pivots.reshape(-1)
    line_index = flat_pivots // cols_all
    column = flat_pivots % cols_all
    offset = line_index - lax.axis_index("row") * line_dev
    inside = (offset >= 0) & (offset < line_dev)
    position = jnp.clip(offset, 0, line_dev - 1) * cols_all + column
    picked = jnp.take(band_images.reshape(band_dev, line_dev * cols_all), position, axis=1)
    picked = jnp.where(inside[None, :], picked, jnp.zeros_like(picked))
    stacked = lax.all_gather(picked, "pix", axis=0, tiled=True)
    spectra = lax.psum(stacked.astype(jnp.float32).astype(jnp.bfloat16), "row").astype(jnp.float32)
    basis = orthonormal(spectra.T)
    shaped = band_images.reshape(band_dev, line_dev, pix_count, row_count, narrow)
    arrived = lax.all_to_all(
        lax.all_to_all(shaped, "pix", split_axis=2, concat_axis=0, tiled=True),
        "row",
        split_axis=3,
        concat_axis=1,
        tiled=True,
    )
    block = (
        arrived.reshape(arrived.shape[0], arrived.shape[1], narrow)
        .transpose(2, 1, 0)
        .astype(jnp.float32)
    )
    return project(block, basis)


def solution(mesh):
    placed = (P("pix", "row", None), P())
    return jax.shard_map(
        shards,
        mesh=mesh,
        in_specs=placed,
        out_specs=(P(("pix", "row"), None, None), P(None, ("pix", "row"), None)),
        check_vma=False,
    )
```

profile of v0, /device:TPU:2, one launch (start us, length us, event | category | flops | bytes accessed | tf_op | source)
XLA Modules:
  0.0 110.3 jit_solution(18243196905711492691)
XLA Ops:
  0.6 4.6 %copy.18 = bf16[32,32,512]{1,2,0:T(8,128)(2,1)} copy(bf16[32,32,512]{2,1,0:T(8,128)(2,1)} %param.2) | data formatting | bytes 2097152 | tf_op args[0]
  5.2 5.5 %copy.30 = bf16[32,32,8,4,16]{1,4,3,0,2:T(8,128)(2,1)} copy(bf16[32,32,8,4,16]{1,4,3,2,0:T(8,128)(2,1)} %bitcast.51) | data formatting | bytes 2097152 | tf_op jit(solution)/shard_map/reshape | solution.py:45
  10.7 7.8 %reshape.198 = bf16[8,2,32768]{2,1,0:T(2,128)(2,1)} reshape(bf16[8,32,4,16,32]{4,3,2,1,0:T(8,128)(2,1)} %bitcast.50) | data formatting | bytes 2097152
  18.5 4.4 %all-to-all-start = ((bf16[8,2,32768]{2,1,0:T(2,128)(2,1)}), bf16[8,2,32768]{2,1,0:T(2,128)(2,1)S(1)}, u32[]{:S(2)}, u32[]{:S(2)}) async-start(bf16[8,2,32768]{2,1,0:T(2,128)(2,1)} %reshape.198), calls=%async_computation | async-start | bytes 2097152 | tf_op jit(solution)/shard_map/all_to_all | solution.py:47
  22.9 0.0 copy-done
  22.9 3.3 %copy.23 = bf16[32,32,512]{0,2,1:T(8,128)(2,1)} copy(bf16[32,32,512]{2,1,0:T(8,128)(2,1)S(1)} %copy-done) | data formatting | bytes 2097152 | tf_op args[0]
  26.2 0.0 copy-done.1
  26.2 0.1 reshape.187
  26.3 0.1 reshape.185
  26.4 3.3 %gather_fusion = bf16[64,32]{1,0:T(8,128)(2,1)S(1)} fusion(bf16[32,16384]{0,1:T(8,128)(2,1)} %bitcast.54, s32[1024]{0:T(1024)S(1)} %pad_clamp_fusion), kind=kCustom, calls=%fused_computation | custom fusion | bytes 8448 | tf_op jit(solution)/shard_map/jit(_take)/gather | solution.py:40
  29.8 7.0 %all-to-all-done = bf16[8,2,32768]{2,1,0:T(2,128)(2,1)S(1)} async-done(((bf16[8,2,32768]{2,1,0:T(2,128)(2,1)}), bf16[8,2,32768]{2,1,0:T(2,128)(2,1)S(1)}, u32[]{:S(2)}, u32[]{:S(2)}) %all-to-all-start) | async-done | bytes 1048608 | tf_op jit(solution)/shard_map/all_to_all | solution.py:47
  36.8 4.5 %reshape.199 = bf16[8,32,4,16,32]{4,3,2,1,0:T(8,128)(2,1)} reshape(bf16[8,2,32768]{2,1,0:T(2,128)(2,1)S(1)} %all-to-all-done) | data formatting | bytes 2097152
  41.3 6.9 %copy.21 = bf16[256,32,1,4,16]{0,4,1,2,3:T(8,128)(2,1)} copy(bf16[256,32,1,4,16]{1,4,3,0,2:T(8,128)(2,1)} %bitcast.49) | data formatting | bytes 2097152 | tf_op jit(solution)/shard_map/all_to_all | solution.py:47
  48.3 4.9 %all-to-all-start.1 = ((bf16[256,32,1,4,16]{0,4,1,2,3:T(8,128)(2,1)}), bf16[256,32,1,4,16]{0,4,1,2,3:T(8,128)(2,1)S(1)}, u32[]{:S(2)}, u32[]{:S(2)}) async-start(bf16[256,32,1,4,16]{0,4,1,2,3:T(8,128)(2,1)} %copy.21), calls=%async_computation.1 | async-start | bytes 2097152 | tf_op jit(solution)/shard_map/all_to_all | solution.py:46
  53.1 0.1 select_bitcast_fusion
  53.2 0.1 copy.24
  53.3 9.2 %all_gather.3 = bf16[256,64]{1,0:T(8,128)(2,1)S(1)} all-gather(bf16[32,64]{1,0:T(8,128)(2,1)S(1)} %copy.24), channel_id=1, replica_groups=mesh['pix'=8,'row'=4] {'pix'}, dimensions={0}, use_global_device_ids=true | all-gather | bytes 36864 | tf_op jit(solution)/shard_map/all_gather | solution.py:42
  62.6 26.2 %psum.7 = bf16[256,64]{1,0:T(8,128)(2,1)S(1)} all-reduce(bf16[256,64]{1,0:T(8,128)(2,1)S(1)} %all_gather.3), channel_id=1, replica_groups=mesh['pix'=8,'row'=4] {'row'}, use_global_device_ids=true, to_apply=%region_0.1 | all-reduce | flops 16384 | bytes 65536 | tf_op jit(solution)/shard_map/psum | solution.py:43
  88.8 0.2 fusion.13
  89.0 0.1 copy.25
  89.0 5.8 %cholesky.16 = f32[64,64]{1,0:T(8,128)S(1)} custom-call(f32[64,64]{1,0:T(8,128)S(1)} %fusion.3), custom_call_target="Cholesky" | custom-call | tf_op jit(solution)/shard_map/jit(cholesky)/cholesky | solution.py:11
  94.9 0.6 compare_reduce_fusion
  95.6 0.7 fusion
  96.2 4.9 %custom-call.7 = f32[1,64,64]{1,2,0:T(8,128)S(1)} custom-call(f32[1,64,64]{2,1,0:T(8,128)S(1)} %fusion), custom_call_target="InvertDiagBlocksLowerTriangular" | custom-call | tf_op jit(solution)/shard_map/jit(_solve_triangular)/triangular_solve | solution.py:12
  101.1 0.3 fusion.1
  101.4 0.0 all-to-all-done.1
  101.4 0.3 copy.22
  101.8 1.0 fusion.12
  102.8 1.8 %convert_subtract_fusion = f32[16,128,256]{2,1,0:T(8,128)S(1)} fusion(bf16[16,128,256]{2,1,0:T(8,128)(2,1)S(1)} %bitcast.53, f32[32,16,128]{2,0,1:T(8,128)S(1)} %get-tuple-element.15, f32[64,256]{1,0:T(8,128)S(1)} %fusion.1), kind=kOutput, calls=%fused_computation.2 | convolution fusion | flops 202375168 | bytes 3440640 | tf_op jit(solution)/shard_map/kcl,kb->clb/dot_general | solution.py:20
  104.6 2.0 %fusion.11 = (bf16[32,16,128]{2,0,1:T(8,128)(2,1)S(1)}, f32[32,16,128]{2,0,1:T(8,128)S(1)}) fusion(f32[16,128,256]{2,1,0:T(8,128)S(1)} %convert_subtract_fusion, f32[64,256]{1,0:T(8,128)S(1)} %fusion.1), kind=kOutput, calls=%fused_computation.38 | convolution fusion | flops 201392128 | bytes 2523136 | tf_op jit(solution)/shard_map/clb,kb->kcl/dot_general | solution.py:21
  106.6 2.8 %subtract_convert_fusion = bf16[16,128,256]{2,1,0:T(8,128)(2,1)} fusion(f32[16,128,256]{2,1,0:T(8,128)S(1)} %convert_subtract_fusion, f32[32,16,128]{2,0,1:T(8,128)S(1)} %get-tuple-element.13, f32[64,256]{1,0:T(8,128)S(1)} %fusion.1), kind=kOutput, calls=%fused_computation.1 | convolution fusion | flops 202375168 | bytes 3440640 | tf_op jit(solution)/shard_map/kcl,kb->clb/dot_general | solution.py:22
  109.5 0.9 copy.26
  (9 shorter events, 0.1 us)
Async XLA Ops:
  18.5 4.4 %copy-start = (bf16[32,32,512]{2,1,0:T(8,128)(2,1)S(1)}, bf16[32,32,512]{2,1,0:T(8,128)(2,1)}, u32[]{:S(2)}) copy-start(bf16[32,32,512]{2,1,0:T(8,128)(2,1)} %param.2) | copy-start | bytes 3145732
  18.5 18.3 %all-to-all-start = ((bf16[8,2,32768]{2,1,0:T(2,128)(2,1)}), bf16[8,2,32768]{2,1,0:T(2,128)(2,1)S(1)}, u32[]{:S(2)}, u32[]{:S(2)}) async-start(bf16[8,2,32768]{2,1,0:T(2,128)(2,1)} %reshape.198), calls=%async_computation | async-start | bytes 2097152 | tf_op jit(solution)/shard_map/all_to_all | solution.py:47
  22.9 3.3 %copy-start.1 = (s32[2,32]{1,0:T(2,128)S(1)}, s32[2,32]{1,0:T(2,128)}, u32[]{:S(2)}) copy-start(s32[2,32]{1,0:T(2,128)} %param.3) | copy-start | bytes 772
  48.3 53.1 %all-to-all-start.1 = ((bf16[256,32,1,4,16]{0,4,1,2,3:T(8,128)(2,1)}), bf16[256,32,1,4,16]{0,4,1,2,3:T(8,128)(2,1)S(1)}, u32[]{:S(2)}, u32[]{:S(2)}) async-start(bf16[256,32,1,4,16]{0,4,1,2,3:T(8,128)(2,1)} %copy.21), calls=%async_computation.1 | async-start | bytes 2097152 | tf_op jit(solution)/shard_map/all_to_all | solution.py:46
where the time goes:
time: 111 us; the launch traced here: 110 us
  local copies, waits for them, and re-layouts  37.5 us (34%)
  blocking collectives  35.5 us (32%)
  other arithmetic  12.2 us (11%)
  starting transfers between devices  9.26 us (8%)
  matrix products  8.1 us (7%)
  waiting for transfers between devices  7.03 us (6%)
    psum x1, blocking collectives, shards(): lax.psum(stacked.astype(jnp.float32).astype(jnp.bfloat16), 'row')  26.2 us
    unnamed x9, local copies, waits for them, and re-layouts  21.1 us
    all_gather x1, blocking collectives, shards(): stacked = lax.all_gather(picked, 'pix', axis=0, tiled=True)  9.24 us
    all_to_all x1, waiting for transfers between devices, shards(): lax.all_to_all(shaped, 'pix', split_axis=2, concat_axis=0, tiled=True)  7.02 us
    all_to_all x1, local copies, waits for them, and re-layouts, shards(): lax.all_to_all(shaped, 'pix', split_axis=2, concat_axis=0, tiled=True)  6.94 us
    another operation x3, other arithmetic, orthonormal(): factor = jnp.linalg.cholesky(gram)  6.52 us
    another operation x2, other arithmetic, orthonormal(): return jax.scipy.linalg.solve_triangular(factor, spectra, lower=True)  5.55 us
    reshape x1, local copies, waits for them, and re-layouts, shards(): band_images.reshape(band_dev, line_dev, pix_count, row_count, narrow)  5.5 us
  transfers between devices with their start and end apart: 2, of which 1 were waited for; matrix products, arithmetic and copies ran while one was open for 18% of the time, Pallas kernels for 0%

commit v1 on v0

v1 whole, which is shorter than its diff:
```python
import jax
import jax.numpy as jnp
from jax import lax
from jax.experimental import pallas as pl
from jax.experimental.pallas import tpu as pltpu
from jax.sharding import PartitionSpec as P

highest = lax.Precision.HIGHEST
f32 = jnp.float32
bf16 = jnp.bfloat16
LANES = 128
SUBLANES = 8
AXES = ("pix", "row")


def contract_last(a, b):
    return lax.dot_general(a, b, (((1,), (1,)), ((), ())), preferred_element_type=f32)


def pack(band_images, column, inner, part_count):
    band_dev, line_dev, cols = band_images.shape
    rows = band_dev * line_dev
    taken = LANES // band_dev
    groups = line_dev // taken
    pivot_count = column.shape[0]
    half = band_dev // 2
    col_step = 2 * LANES

    def kernel(x_ref, col_ref, in_ref, out_ref, spec_ref, wide_ref, rows_ref):
        for c in range(cols // LANES):
            wide_ref[c] = (
                x_ref[:, :, c * LANES : (c + 1) * LANES].astype(f32).reshape(rows, LANES)
            )
        for c in range(cols // LANES):
            for g in range(groups):
                for t in range(taken):
                    line = t * groups + g
                    start = (g * taken + t) * band_dev
                    part = wide_ref[c, pl.ds(line, band_dev, stride=line_dev), :]
                    rows_ref[start : start + band_dev, c * LANES : (c + 1) * LANES] = part.astype(bf16)
        picked = jnp.zeros((pivot_count, rows), f32)
        eye = (
            lax.broadcasted_iota(jnp.int32, (col_step, col_step), 0)
            == lax.broadcasted_iota(jnp.int32, (col_step, col_step), 1)
        ).astype(f32).astype(bf16)
        for c in range(cols // col_step):
            block = rows_ref[:, c * col_step : (c + 1) * col_step]
            hot = (
                lax.broadcasted_iota(jnp.int32, (pivot_count, col_step), 1) + c * col_step
                == col_ref[...]
            ).astype(f32).astype(bf16)
            both = contract_last(jnp.concatenate([eye, hot], axis=0), block)
            out_ref[c * col_step : (c + 1) * col_step, :] = both[:col_step].astype(bf16)
            picked = picked + both[col_step:]
        lane = lax.broadcasted_iota(jnp.int32, (pivot_count, rows), 1)
        piece = lane // band_dev
        line = (piece % taken) * groups + piece // taken
        picked = jnp.where(line == in_ref[...], picked, 0.0).astype(bf16)
        fold = (
            lax.broadcasted_iota(jnp.int32, (band_dev, rows), 1) % band_dev
            == lax.broadcasted_iota(jnp.int32, (band_dev, rows), 0)
        ).astype(f32).astype(bf16)
        found = contract_last(fold, picked)
        found = jnp.concatenate([found[:half], found[half:]], axis=1).astype(bf16)
        spec_ref[...] = jnp.broadcast_to(found[None], spec_ref.shape)

    return pl.pallas_call(
        kernel,
        out_shape=(
            jax.ShapeDtypeStruct((cols, rows), bf16),
            jax.ShapeDtypeStruct((part_count, half, 2 * pivot_count), bf16),
        ),
        scratch_shapes=[
            pltpu.VMEM((cols // LANES, rows, LANES), f32),
            pltpu.VMEM((rows, cols), bf16),
        ],
        name="pack",
    )(band_images, column, inner)


def finish(arrived, keep, gains, pix_count, row_count, band_dev, line_dev):
    sources, narrow, rows = arrived.shape
    taken = LANES // band_dev
    groups = line_dev // taken
    lines = row_count * line_dev
    bands = pix_count * band_dev
    kept = gains.shape[0] // 2
    width = 4
    joined = bands // LANES

    def swap(low, high, shift, mask):
        return (
            jnp.where(mask, low, pltpu.roll(high, shift, 1)),
            jnp.where(mask, pltpu.roll(low, LANES - shift, 1), high),
        )

    def kernel(a_ref, keep_ref, gain_ref, res_ref, coef_ref, wide_ref, x_ref, hold_ref):
        for s in range(sources):
            for g in range(rows // LANES):
                wide_ref[s * (rows // LANES) + g] = a_ref[s, :, g * LANES : (g + 1) * LANES].astype(f32)
        flat = wide_ref.reshape(sources * (rows // LANES) * narrow, LANES)
        lane = lax.broadcasted_iota(jnp.int32, (SUBLANES, LANES), 1)
        for c in range(narrow):
            for r in range(row_count):
                for j in range(joined):
                    v = []
                    for i in range(taken):
                        source = (j * taken + i) * row_count + r
                        v.append(flat[pl.ds(source * (rows // LANES) * narrow + c, groups, stride=narrow), :])
                    step = taken // 2
                    while step >= 1:
                        shift = step * band_dev
                        mask = (lane // shift) % 2 == 0
                        w = list(v)
                        for i in range(taken):
                            if (i // step) % 2 == 0:
                                w[i], w[i + step] = swap(v[i], v[i + step], shift, mask)
                        v = w
                        step //= 2
                    row = c * lines + r * line_dev
                    x_ref[row : row + line_dev, j * LANES : (j + 1) * LANES] = (
                        jnp.concatenate(v, axis=0).astype(bf16)
                    )
        for s in range(0, narrow, width):
            pixels = x_ref[s * lines : (s + width) * lines, :]
            both = jnp.dot(pixels, keep_ref[:bands], preferred_element_type=f32)
            both = both + jnp.dot(pixels, keep_ref[bands:], preferred_element_type=f32)
            res_ref[s : s + width] = both.astype(bf16).reshape(width, lines, bands)
            found = contract_last(gain_ref[...], pixels)
            found = found[:kept] + found[kept:]
            for i in range(width):
                hold_ref[:, s + i, :] = found[:, i * lines : (i + 1) * lines]
        coef_ref[...] = hold_ref[...].astype(bf16)

    return pl.pallas_call(
        kernel,
        out_shape=(
            jax.ShapeDtypeStruct((narrow, lines, bands), bf16),
            jax.ShapeDtypeStruct((kept, narrow, lines), bf16),
        ),
        scratch_shapes=[
            pltpu.VMEM((sources * (rows // LANES), narrow, LANES), f32),
            pltpu.VMEM((narrow * lines, bands), bf16),
            pltpu.VMEM((kept, narrow, lines), f32),
        ],
        name="finish",
    )(arrived, keep, gains)


def split(a):
    high = lax.reduce_precision(a, 8, 7)
    return jnp.concatenate([high, a - high], axis=0).astype(bf16)


def orthonormal(spectra):
    gram = jnp.dot(spectra, spectra.T, precision=highest)
    factor = jnp.linalg.cholesky(gram)
    return jax.scipy.linalg.solve_triangular(factor, spectra, lower=True)


def operators(basis):
    count = basis.shape[0] // 2
    first = basis[:count]
    second = basis[count:]
    cross = jnp.dot(second, first.T, precision=highest)
    second_gain = second - jnp.dot(cross, first, precision=highest)
    gains = jnp.concatenate([first, second_gain], axis=0)
    keep = jnp.eye(basis.shape[1], dtype=f32) - jnp.dot(gains.T, basis, precision=highest)
    return keep, gains


def project(block, basis):
    count = basis.shape[0] // 2
    first = basis[:count]
    second = basis[count:]
    coef_one = jnp.einsum("clb,kb->kcl", block, first, precision=highest)
    remain = block - jnp.einsum("kcl,kb->clb", coef_one, first, precision=highest)
    coef_two = jnp.einsum("clb,kb->kcl", remain, second, precision=highest)
    remain = remain - jnp.einsum("kcl,kb->clb", coef_two, second, precision=highest)
    return (
        remain.astype(bf16),
        jnp.concatenate([coef_one, coef_two], axis=0).astype(bf16),
    )


def plain(band_images, line_index, column, pix_count, row_count, narrow):
    band_dev, line_dev, cols_all = band_images.shape
    offset = line_index - lax.axis_index("row") * line_dev
    inside = (offset >= 0) & (offset < line_dev)
    position = jnp.clip(offset, 0, line_dev - 1) * cols_all + column
    picked = jnp.take(band_images.reshape(band_dev, line_dev * cols_all), position, axis=1)
    picked = jnp.where(inside[None, :], picked, jnp.zeros_like(picked))
    stacked = lax.all_gather(picked, "pix", axis=0, tiled=True)
    spectra = lax.psum(stacked.astype(f32).astype(bf16), "row").astype(f32)
    basis = orthonormal(spectra.T)
    shaped = band_images.reshape(band_dev, line_dev, pix_count, row_count, narrow)
    arrived = lax.all_to_all(
        lax.all_to_all(shaped, "pix", split_axis=2, concat_axis=0, tiled=True),
        "row",
        split_axis=3,
        concat_axis=1,
        tiled=True,
    )
    block = (
        arrived.reshape(arrived.shape[0], arrived.shape[1], narrow)
        .transpose(2, 1, 0)
        .astype(f32)
    )
    return project(block, basis)


def shards(band_images, pivots):
    band_dev, line_dev, cols_all = band_images.shape
    pix_count = lax.axis_size("pix")
    row_count = lax.axis_size("row")
    part_count = pix_count * row_count
    narrow = cols_all // part_count
    flat_pivots = pivots.reshape(-1)
    pivot_count = flat_pivots.shape[0]
    line_index = flat_pivots // cols_all
    column = flat_pivots % cols_all
    lines = row_count * line_dev
    bands = pix_count * band_dev
    taken = LANES // band_dev
    fits = (
        taken * band_dev == LANES
        and taken in (1, 2, 4, 8)
        and line_dev == SUBLANES * taken
        and narrow % 16 == 0
        and cols_all % (2 * LANES) == 0
        and lines == LANES
        and bands % LANES == 0
        and 2 * pivot_count == LANES
    )
    if not fits:
        return plain(band_images, line_index, column, pix_count, row_count, narrow)
    inner = line_index - lax.axis_index("row") * line_dev
    packed, picked = pack(band_images, column[:, None], inner[:, None], part_count)
    spectra = lax.all_to_all(picked, AXES, 0, 0, tiled=True)
    spectra = spectra.astype(f32).reshape(pix_count, row_count, band_dev // 2, 2, pivot_count).sum(1)
    spectra = spectra.transpose(3, 0, 2, 1).reshape(pivot_count, bands)
    basis = orthonormal(spectra)
    keep, gains = operators(basis)
    arrived = lax.all_to_all(packed.reshape(part_count, narrow, line_dev * band_dev), AXES, 0, 0, tiled=True)
    return finish(arrived, split(keep), split(gains), pix_count, row_count, band_dev, line_dev)


def solution(mesh):
    placed = (P("pix", "row", None), P())
    return jax.shard_map(
        shards,
        mesh=mesh,
        in_specs=placed,
        out_specs=(P(AXES, None, None), P(None, AXES, None)),
        check_vma=False,
    )
```

time: 111 us -> 56.6 us (0.51)
  the two profiles are of different devices: /device:TPU:2 before, /device:TPU:1 now
where the time goes in v1:
time: 56.6 us; the launch traced here: 56.3 us
  blocking collectives  14.5 us (26%)
  other arithmetic  14.4 us (25%)
  waiting for transfers between devices  10.8 us (19%)
  Pallas kernels  8.78 us (16%)
  starting transfers between devices  3.51 us (6%)
  local copies, waits for them, and re-layouts  2.16 us (4%)
  matrix products  1.43 us (3%)
  between operations  0.76 us (1%)
    all_to_all x1, blocking collectives, shards(): spectra = lax.all_to_all(picked, AXES, 0, 0, tiled=True)  14.5 us
    all_to_all x1, waiting for transfers between devices, shards(): lax.all_to_all(packed.reshape(part_count, narrow, line_dev * band_dev), A...  10.8 us
    another operation x3, other arithmetic, orthonormal(): factor = jnp.linalg.cholesky(gram)  6.52 us
    another operation x2, other arithmetic, orthonormal(): return jax.scipy.linalg.solve_triangular(factor, spectra, lower=True)  5.55 us
    pallas_call x1, Pallas kernels, finish(): pl.pallas_call(kernel, out_shape=(jax.ShapeDtypeStruct((narrow, lines, ba...  4.57 us
    pallas_call x1, Pallas kernels, pack(): pl.pallas_call(kernel, out_shape=(jax.ShapeDtypeStruct((cols, rows), bf16...  4.21 us
    all_to_all x1, starting transfers between devices, shards(): lax.all_to_all(packed.reshape(part_count, narrow, line_dev * band_dev), A...  3.51 us
    unnamed x4, local copies, waits for them, and re-layouts  1.66 us
  transfers between devices with their start and end apart: 1, of which 1 were waited for; matrix products, arithmetic and copies ran while one was open for 28% of the time, Pallas kernels for 0%

profile of v1, /device:TPU:1, one launch (start us, length us, event | category | flops | bytes accessed | tf_op | source)
XLA Modules:
  0.0 56.3 jit_solution(8846800306219092479)
XLA Ops:
  0.6 0.0 copy-start.1
  0.6 0.7 %copy-done.1 = s32[2,32]{1,0:T(2,128)S(1)} copy-done((s32[2,32]{1,0:T(2,128)S(1)}, s32[2,32]{1,0:T(2,128)}, u32[]{:S(2)}) %copy-start.1) | copy-done | bytes 280
  1.3 0.1 reshape.142
  1.4 0.7 %fusion.3 = (s32[64,1]{1,0:T(8,128)}, s32[64,1]{1,0:T(8,128)}) fusion(s32[64,1]{1,0:T(8,128)S(1)} %reshape.142, s32[]{:T(128)S(6)} %mul.3), kind=kLoop, calls=%fused_computation.20 | loop fusion | flops 1280 | bytes 772 | tf_op jit(solution)/shard_map/sub | solution.py:237
  2.1 4.2 %pack.1 = (bf16[512,1024]{1,0:T(8,128)(2,1)}, bf16[32,16,128]{2,1,0:T(8,128)(2,1)}) custom-call(bf16[32,32,512]{2,1,0:T(8,128)(2,1)} %x_ref.1, s32[64,1]{1,0:T(8,128)} %get-tuple-element.11.col_ref, s32[64,1]{1,0:T(8,128)} %get-tuple-element.10.in_ref), custom_call_target="tpu_custom_call" | custom-call | tf_op jit(solution)/shard_map/pack/pallas_call | solution.py:67
  6.3 14.5 %all_to_all.10 = bf16[32,16,128]{2,1,0:T(8,128)(2,1)S(1)} all-to-all(bf16[32,16,128]{2,1,0:T(8,128)(2,1)} %get-tuple-element.5), channel_id=1, replica_groups=mesh['pix'=8,'row'=4] {'pix','row'}, dimensions={0} | all-to-all | bytes 262144 | tf_op jit(solution)/shard_map/all_to_all | solution.py:239
  20.8 3.5 %all-to-all-start = ((bf16[32,16,1024]{2,1,0:T(8,128)(2,1)}), bf16[32,16,1024]{2,1,0:T(8,128)(2,1)S(1)}, u32[]{:S(2)}, u32[]{:S(2)}) async-start(bf16[32,16,1024]{2,1,0:T(8,128)(2,1)} %bitcast.19), calls=%async_computation | async-start | bytes 2097152 | tf_op jit(solution)/shard_map/all_to_all | solution.py:244
  24.3 0.3 reshape.140
  24.6 0.3 reduce_sum.9
  24.9 0.4 convolution_bitcast_fusion
  25.3 0.1 copy.22
  25.4 5.8 %cholesky.16 = f32[64,64]{1,0:T(8,128)S(1)} custom-call(f32[64,64]{1,0:T(8,128)S(1)} %fusion.6), custom_call_target="Cholesky" | custom-call | tf_op jit(solution)/shard_map/jit(cholesky)/cholesky | solution.py:157
  31.3 0.6 %compare_reduce_fusion = pred[]{:T(512)} fusion(f32[64]{0:T(128)S(1)} %select_reduce_fusion), kind=kLoop, calls=%fused_computation.33 | loop fusion | flops 127 | bytes 257 | tf_op jit(solution)/shard_map/jit(cholesky)/cholesky | solution.py:157
  31.9 0.7 %fusion.2 = f32[1,64,64]{2,1,0:T(8,128)S(1)} fusion(f32[64,64]{1,0:T(8,128)S(1)} %cholesky.16, pred[]{:T(512)} %compare_reduce_fusion), kind=kLoop, calls=%fused_computation.19 | loop fusion | flops 16384 | bytes 32769 | tf_op jit(solution)/shard_map/jit(_solve_triangular)/triangular_solve | solution.py:158
  32.6 4.9 %custom-call.7 = f32[1,64,64]{1,2,0:T(8,128)S(1)} custom-call(f32[1,64,64]{2,1,0:T(8,128)S(1)} %fusion.2), custom_call_target="InvertDiagBlocksLowerTriangular" | custom-call | tf_op jit(solution)/shard_map/jit(_solve_triangular)/triangular_solve | solution.py:158
  37.5 0.3 fusion.4
  37.8 0.2 fusion.8
  38.0 0.2 convolution_subtract_fusion.1
  38.2 0.6 %pad_maximum_fusion.2.gain_ref = bf16[128,256]{1,0:T(8,128)(2,1)} fusion(bf16[64,256]{1,0:T(8,128)(2,1)S(1)} %get-tuple-element.9, bf16[64,256]{1,0:T(8,128)(2,1)S(1)} %get-tuple-element.8), kind=kLoop, calls=%fused_computation.12 | loop fusion | flops 131072 | bytes 131072 | tf_op jit(solution)/shard_map/concatenate | solution.py:152
  38.8 0.4 reduce-precision_convert_fusion
  39.2 0.7 %pad_maximum_fusion.keep_ref = bf16[512,256]{1,0:T(8,128)(2,1)} fusion(bf16[256,256]{1,0:T(8,128)(2,1)S(1)} %get-tuple-element.7, bf16[256,256]{1,0:T(8,128)(2,1)S(1)} %get-tuple-element.6), kind=kLoop, calls=%fused_computation.6 | loop fusion | flops 524288 | bytes 524288 | tf_op jit(solution)/shard_map/concatenate | solution.py:152
  40.0 10.8 %all-to-all-done.a_ref = bf16[32,16,1024]{2,1,0:T(8,128)(2,1)S(1)} async-done(((bf16[32,16,1024]{2,1,0:T(8,128)(2,1)}), bf16[32,16,1024]{2,1,0:T(8,128)(2,1)S(1)}, u32[]{:S(2)}, u32[]{:S(2)}) %all-to-all-start) | async-done | bytes 1048608 | tf_op jit(solution)/shard_map/all_to_all | solution.py:244
  50.7 0.0 copy-start
  50.7 1.0 %copy-done = bf16[32,16,1024]{2,1,0:T(8,128)(2,1)} copy-done((bf16[32,16,1024]{2,1,0:T(8,128)(2,1)}, bf16[32,16,1024]{2,1,0:T(8,128)(2,1)S(1)}, u32[]{:S(2)}) %copy-start) | copy-done | bytes 1048600
  51.7 4.6 %finish.1 = (bf16[16,128,256]{2,1,0:T(8,128)(2,1)}, bf16[64,16,128]{2,1,0:T(8,128)(2,1)}) custom-call(bf16[32,16,1024]{2,1,0:T(8,128)(2,1)} %copy-done, bf16[512,256]{1,0:T(8,128)(2,1)} %pad_maximum_fusion.keep_ref, bf16[128,256]{1,0:T(8,128)(2,1)} %pad_maximum_fusion.2.gain_ref), custom_call_target="tpu_custom_call" | custom-call | tf_op jit(solution)/shard_map/finish/pallas_call | solution.py:135
  (5 shorter events, 0.1 us)
Async XLA Ops:
  0.6 0.7 %copy-start.1 = (s32[2,32]{1,0:T(2,128)S(1)}, s32[2,32]{1,0:T(2,128)}, u32[]{:S(2)}) copy-start(s32[2,32]{1,0:T(2,128)} %param.3) | copy-start | bytes 772
  20.8 30.0 %all-to-all-start = ((bf16[32,16,1024]{2,1,0:T(8,128)(2,1)}), bf16[32,16,1024]{2,1,0:T(8,128)(2,1)S(1)}, u32[]{:S(2)}, u32[]{:S(2)}) async-start(bf16[32,16,1024]{2,1,0:T(8,128)(2,1)} %bitcast.19), calls=%async_computation | async-start | bytes 2097152 | tf_op jit(solution)/shard_map/all_to_all | solution.py:244
  50.7 1.0 %copy-start = (bf16[32,16,1024]{2,1,0:T(8,128)(2,1)}, bf16[32,16,1024]{2,1,0:T(8,128)(2,1)S(1)}, u32[]{:S(2)}) copy-start(bf16[32,16,1024]{2,1,0:T(8,128)(2,1)S(1)} %all-to-all-done.a_ref) | copy-start | bytes 3145732

commit v2 on v1

--- a/solution.py
+++ b/solution.py
@@ -5,6 +5,7 @@
 from jax.experimental.pallas import tpu as pltpu
 from jax.sharding import PartitionSpec as P
 
+
 highest = lax.Precision.HIGHEST
 f32 = jnp.float32
 bf16 = jnp.bfloat16
@@ -17,65 +18,71 @@
     return lax.dot_general(a, b, (((1,), (1,)), ((), ())), preferred_element_type=f32)
 
 
-def pack(band_images, column, inner, part_count):
+def pick(band_images, pivots, row_index):
+    band_dev, line_dev, cols = band_images.shape
+    rows = band_dev * line_dev
+    panels, panel = pivots.shape
+    pivot_count = panels * panel
+    shift = cols.bit_length() - 1
+
+    def kernel(row_ref, x_ref, piv_ref, spec_ref):
+        flat = jnp.concatenate([piv_ref[i : i + 1, :] for i in range(panels)], axis=1)
+        column = flat & (cols - 1)
+        inner = (flat >> shift) - row_ref[0] * line_dev
+        hot = (
+            lax.broadcasted_iota(jnp.int32, (cols, pivot_count), 0) == column
+        ).astype(f32).astype(bf16)
+        found = jnp.dot(x_ref[...].reshape(rows, cols), hot, preferred_element_type=f32)
+        line = lax.broadcasted_iota(jnp.int32, (line_dev, pivot_count), 0)
+        found = jnp.where((line == inner)[None], found.reshape(band_dev, line_dev, pivot_count), 0.0)
+        spec_ref[...] = jnp.sum(found, axis=1).astype(bf16)
+
+    return pl.pallas_call(
+        kernel,
+        out_shape=jax.ShapeDtypeStruct((band_dev, pivot_count), bf16),
+        in_specs=[
+            pl.BlockSpec(memory_space=pltpu.SMEM),
+            pl.BlockSpec(memory_space=pltpu.VMEM),
+            pl.BlockSpec(memory_space=pltpu.VMEM),
+        ],
+        name="pick",
+    )(row_index, band_images, pivots)
+
+
+def pack(band_images):
     band_dev, line_dev, cols = band_images.shape
     rows = band_dev * line_dev
     taken = LANES // band_dev
     groups = line_dev // taken
-    pivot_count = column.shape[0]
-    half = band_dev // 2
     col_step = 2 * LANES
 
-    def kernel(x_ref, col_ref, in_ref, out_ref, spec_ref, wide_ref, rows_ref):
+    def kernel(x_ref, out_ref, wide_ref, rows_ref):
+        eye = (
+            lax.broadcasted_iota(jnp.int32, (col_step, col_step), 0)
+            == lax.broadcasted_iota(jnp.int32, (col_step, col_step), 1)
+        ).astype(f32).astype(bf16)
         for c in range(cols // LANES):
-            wide_ref[c] = (
-                x_ref[:, :, c * LANES : (c + 1) * LANES].astype(f32).reshape(rows, LANES)
-            )
-        for c in range(cols // LANES):
+            lanes = slice(c * LANES, (c + 1) * LANES)
+            wide_ref[c] = x_ref[:, :, lanes].astype(f32).reshape(rows, LANES)
             for g in range(groups):
                 for t in range(taken):
                     line = t * groups + g
                     start = (g * taken + t) * band_dev
                     part = wide_ref[c, pl.ds(line, band_dev, stride=line_dev), :]
-                    rows_ref[start : start + band_dev, c * LANES : (c + 1) * LANES] = part.astype(bf16)
-        picked = jnp.zeros((pivot_count, rows), f32)
-        eye = (
-            lax.broadcasted_iota(jnp.int32, (col_step, col_step), 0)
-            == lax.broadcasted_iota(jnp.int32, (col_step, col_step), 1)
-        ).astype(f32).astype(bf16)
-        for c in range(cols // col_step):
-            block = rows_ref[:, c * col_step : (c + 1) * col_step]
-            hot = (
-                lax.broadcasted_iota(jnp.int32, (pivot_count, col_step), 1) + c * col_step
-                == col_ref[...]
-            ).astype(f32).astype(bf16)
-            both = contract_last(jnp.concatenate([eye, hot], axis=0), block)
-            out_ref[c * col_step : (c + 1) * col_step, :] = both[:col_step].astype(bf16)
-            picked = picked + both[col_step:]
-        lane = lax.broadcasted_iota(jnp.int32, (pivot_count, rows), 1)
-        piece = lane // band_dev
-        line = (piece % taken) * groups + piece // taken
-        picked = jnp.where(line == in_ref[...], picked, 0.0).astype(bf16)
-        fold = (
-            lax.broadcasted_iota(jnp.int32, (band_dev, rows), 1) % band_dev
-            == lax.broadcasted_iota(jnp.int32, (band_dev, rows), 0)
-        ).astype(f32).astype(bf16)
-        found = contract_last(fold, picked)
-        found = jnp.concatenate([found[:half], found[half:]], axis=1).astype(bf16)
-        spec_ref[...] = jnp.broadcast_to(found[None], spec_ref.shape)
+                    rows_ref[start : start + band_dev, lanes] = part.astype(bf16)
+            if c % 2 == 1:
+                both = slice((c - 1) * LANES, (c + 1) * LANES)
+                out_ref[both, :] = contract_last(eye, rows_ref[:, both]).astype(bf16)
 
     return pl.pallas_call(
         kernel,
-        out_shape=(
-            jax.ShapeDtypeStruct((cols, rows), bf16),
-            jax.ShapeDtypeStruct((part_count, half, 2 * pivot_count), bf16),
-        ),
+        out_shape=jax.ShapeDtypeStruct((cols, rows), bf16),
         scratch_shapes=[
             pltpu.VMEM((cols // LANES, rows, LANES), f32),
             pltpu.VMEM((rows, cols), bf16),
         ],
         name="pack",
-    )(band_images, column, inner)
+    )(band_images)
 
 
 def finish(arrived, keep, gains, pix_count, row_count, band_dev, line_dev):
@@ -144,7 +151,12 @@
             pltpu.VMEM((kept, narrow, lines), f32),
         ],
         name="finish",
-    )(arrived, keep, gains)
+    )(pltpu.with_memory_space_constraint(arrived, pltpu.VMEM), keep, gains)
+
+
+def exchange(x, axis, k):
+    count = lax.axis_size(axis)
+    return lax.ppermute(x, axis, [(i, i ^ k) for i in range(count)])
 
 
 def split(a):
@@ -230,19 +242,27 @@
         and cols_all % (2 * LANES) == 0
         and lines == LANES
         and bands % LANES == 0
-        and 2 * pivot_count == LANES
+        and cols_all & (cols_all - 1) == 0
+        and pix_count & (pix_count - 1) == 0
+        and row_count & (row_count - 1) == 0
     )
     if not fits:
         return plain(band_images, line_index, column, pix_count, row_count, narrow)
-    inner = line_index - lax.axis_index("row") * line_dev
-    packed, picked = pack(band_images, column[:, None], inner[:, None], part_count)
-    spectra = lax.all_to_all(picked, AXES, 0, 0, tiled=True)
-    spectra = spectra.astype(f32).reshape(pix_count, row_count, band_dev // 2, 2, pivot_count).sum(1)
-    spectra = spectra.transpose(3, 0, 2, 1).reshape(pivot_count, bands)
-    basis = orthonormal(spectra)
-    keep, gains = operators(basis)
-    arrived = lax.all_to_all(packed.reshape(part_count, narrow, line_dev * band_dev), AXES, 0, 0, tiled=True)
-    return finish(arrived, split(keep), split(gains), pix_count, row_count, band_dev, line_dev)
+    row_index = lax.axis_index("row").astype(jnp.int32).reshape(1)
+    picked = pick(band_images, pivots, row_index)
+    found = picked
+    for k in range(1, row_count):
+        found = found + exchange(picked, "row", k)
+    packed = pack(band_images).reshape(part_count, narrow, line_dev * band_dev)
+    arrived = lax.all_to_all(packed, AXES, 0, 0, tiled=True)
+    order = found[None]
+    for k in range(pix_count.bit_length() - 1):
+        order = jnp.concatenate([order, exchange(order, "pix", 1 << k)], axis=0)
+    spectra = order.astype(f32)[jnp.arange(pix_count) ^ lax.axis_index("pix")]
+    spectra = spectra.reshape(bands, pivot_count).T
+    keep, gains = operators(orthonormal(spectra))
+    keep, gains = split(keep), split(gains)
+    return finish(arrived, keep, gains, pix_count, row_count, band_dev, line_dev)
 
 
 def solution(mesh):

time: 56.6 us -> 55.2 us (0.975)
  the two profiles are of different devices: /device:TPU:1 before, /device:TPU:0 now
where the time goes in v2:
time: 55.2 us; the launch traced here: 54.9 us
  other arithmetic  14.2 us (26%)
  waiting for transfers between devices  14.1 us (26%)
  starting transfers between devices  13.4 us (24%)
  Pallas kernels  10.6 us (19%)
  matrix products  1.18 us (2%)
  between operations  0.75 us (1%)
  local copies, waits for them, and re-layouts  0.64 us (1%)
    ppermute x6, waiting for transfers between devices, exchange(): return lax.ppermute(x, axis, [(i, i ^ k) for i in range(count)])  14.1 us
    ppermute x6, starting transfers between devices, exchange(): return lax.ppermute(x, axis, [(i, i ^ k) for i in range(count)])  9 us
    another operation x3, other arithmetic, orthonormal(): factor = jnp.linalg.cholesky(gram)  6.52 us
    another operation x2, other arithmetic, orthonormal(): return jax.scipy.linalg.solve_triangular(factor, spectra, lower=True)  5.55 us
    all_to_all x1, starting transfers between devices, shards(): arrived = lax.all_to_all(packed, AXES, 0, 0, tiled=True)  4.39 us
    pallas_call x1, Pallas kernels, finish(): pl.pallas_call(kernel, out_shape=(jax.ShapeDtypeStruct((narrow, lines, ba...  4.19 us
    pallas_call x1, Pallas kernels, pack(): pl.pallas_call(kernel, out_shape=jax.ShapeDtypeStruct((cols, rows), bf16)...  4.1 us
    pallas_call x1, Pallas kernels, pick(): pl.pallas_call(kernel, out_shape=jax.ShapeDtypeStruct((band_dev, pivot_co...  2.34 us
  transfers between devices with their start and end apart: 7, of which 4 were waited for; matrix products, arithmetic and copies ran while one was open for 28% of the time, Pallas kernels for 7%

profile of v2, /device:TPU:0, one launch (start us, length us, event | category | flops | bytes accessed | tf_op | source)
XLA Modules:
  0.0 54.9 jit_solution(10667991581761228933)
XLA Ops:
  0.6 2.3 %pick.1 = bf16[32,64]{1,0:T(8,128)(2,1)} custom-call(s32[1]{0:T(128)} %bitcast.1.row_ref, bf16[32,32,512]{2,1,0:T(8,128)(2,1)} %x_ref.3, s32[2,32]{1,0:T(2,128)} %piv_ref.1), custom_call_target="tpu_custom_call" | custom-call | tf_op jit(solution)/shard_map/pick/pallas_call | solution.py:40
  3.0 5.1 %collective-permute-start.2 = (bf16[32,64]{1,0:T(8,128)(2,1)}, bf16[32,64]{1,0:T(8,128)(2,1)S(1)}, u32[]{:S(2)}, u32[]{:S(2)}) collective-permute-start(bf16[32,64]{1,0:T(8,128)(2,1)} %pick.1), channel_id=1, source_target_pairs={{0,3},{1,2},{2,1},{3,0},{4,7},{5,6},{6,5},{7,4},{8,11},{9,10},{10,... | collective-permute-start | bytes 12296 | tf_op jit(solution)/shard_map/ppermute | solution.py:159
  8.0 0.0 collective-permute-start.1
  8.1 0.6 %collective-permute-start = (bf16[32,64]{1,0:T(8,128)(2,1)}, bf16[32,64]{1,0:T(8,128)(2,1)S(1)}, u32[]{:S(2)}, u32[]{:S(2)}) collective-permute-start(bf16[32,64]{1,0:T(8,128)(2,1)} %pick.1), channel_id=1, source_target_pairs={{0,1},{1,0},{2,3},{3,2},{4,5},{5,4},{6,7},{7,6},{8,9},{9,8},{10,11... | collective-permute-start | bytes 12296 | tf_op jit(solution)/shard_map/ppermute | solution.py:159
  8.6 1.3 %collective-permute-done.2 = bf16[32,64]{1,0:T(8,128)(2,1)S(1)} collective-permute-done((bf16[32,64]{1,0:T(8,128)(2,1)}, bf16[32,64]{1,0:T(8,128)(2,1)S(1)}, u32[]{:S(2)}, u32[]{:S(2)}) %collective-permute-start.2) | collective-permute-done | bytes 4128 | tf_op jit(solution)/shard_map/ppermute | solution.py:159
  9.9 2.9 %collective-permute-done.1 = bf16[32,64]{1,0:T(8,128)(2,1)S(1)} collective-permute-done((bf16[32,64]{1,0:T(8,128)(2,1)}, bf16[32,64]{1,0:T(8,128)(2,1)S(1)}, u32[]{:S(2)}, u32[]{:S(2)}) %collective-permute-start.1) | collective-permute-done | bytes 4128 | tf_op jit(solution)/shard_map/ppermute | solution.py:159
  12.8 0.0 collective-permute-done
  12.8 0.7 %add_bitcast_fusion = bf16[1,32,64]{2,1,0:T(8,128)(2,1)S(1)} fusion(bf16[32,64]{1,0:T(8,128)(2,1)S(1)} %collective-permute-done.2, bf16[32,64]{1,0:T(8,128)(2,1)S(1)} %collective-permute-done.1, bf16[32,64]{1,0:T(8,128)(2,1)} %pick.1, bf16[32,64]{1,0:T(8,128)(2,1)S(1)} %collective-permute-done), kind=kLoop, calls=%fused_computation.28 | loop fusion | flops 6144 | bytes 20480 | tf_op jit(solution)/shard_map/broadcast_in_dim | solution.py:258
  13.5 0.0 collective-permute-start.3
  13.5 4.1 %pack.1 = bf16[512,1024]{1,0:T(8,128)(2,1)} custom-call(bf16[32,32,512]{2,1,0:T(8,128)(2,1)} %x_ref.3), custom_call_target="tpu_custom_call" | custom-call | tf_op jit(solution)/shard_map/pack/pallas_call | solution.py:77
  17.6 4.4 %all-to-all-start = ((bf16[32,16,1024]{2,1,0:T(8,128)(2,1)}), bf16[32,16,1024]{2,1,0:T(8,128)(2,1)S(1)}, u32[]{:S(2)}, u32[]{:S(2)}) async-start(bf16[32,16,1024]{2,1,0:T(8,128)(2,1)} %bitcast.23), calls=%async_computation | async-start | bytes 2097152 | tf_op jit(solution)/shard_map/all_to_all | solution.py:257
  22.0 0.0 collective-permute-done.3
  22.0 1.8 %collective-permute-start.4 = (bf16[2,32,64]{2,1,0:T(8,128)(2,1)S(1)}, bf16[2,32,64]{2,1,0:T(8,128)(2,1)S(1)}, u32[]{:S(2)}, u32[]{:S(2)}) collective-permute-start(bf16[2,32,64]{2,1,0:T(8,128)(2,1)S(1)} %pad_maximum_fusion.6), channel_id=1, source_target_pairs={{0,8},{4,12},{8,0},{12,4},{16,24},{20,28},{24,16},{28,20},{1,9},{5... | collective-permute-start | bytes 24584 | tf_op jit(solution)/shard_map/ppermute | solution.py:159
  23.9 6.5 %collective-permute-done.4 = bf16[2,32,64]{2,1,0:T(8,128)(2,1)S(1)} collective-permute-done((bf16[2,32,64]{2,1,0:T(8,128)(2,1)S(1)}, bf16[2,32,64]{2,1,0:T(8,128)(2,1)S(1)}, u32[]{:S(2)}, u32[]{:S(2)}) %collective-permute-start.4) | collective-permute-done | bytes 8224 | tf_op jit(solution)/shard_map/ppermute | solution.py:159
  30.4 1.5 %collective-permute-start.5 = (bf16[4,32,64]{2,1,0:T(8,128)(2,1)S(1)}, bf16[4,32,64]{2,1,0:T(8,128)(2,1)S(1)}, u32[]{:S(2)}, u32[]{:S(2)}) collective-permute-start(bf16[4,32,64]{2,1,0:T(8,128)(2,1)S(1)} %pad_maximum_fusion.5), channel_id=1, source_target_pairs={{0,16},{4,20},{8,24},{12,28},{16,0},{20,4},{24,8},{28,12},{1,17},{... | collective-permute-start | bytes 49160 | tf_op jit(solution)/shard_map/ppermute | solution.py:159
  31.9 3.4 %collective-permute-done.5 = bf16[4,32,64]{2,1,0:T(8,128)(2,1)S(1)} collective-permute-done((bf16[4,32,64]{2,1,0:T(8,128)(2,1)S(1)}, bf16[4,32,64]{2,1,0:T(8,128)(2,1)S(1)}, u32[]{:S(2)}, u32[]{:S(2)}) %collective-permute-start.5) | collective-permute-done | bytes 16416 | tf_op jit(solution)/shard_map/ppermute | solution.py:159
  35.4 0.6 %gather_fusion = bf16[8,32,64]{2,1,0:T(8,128)(2,1)S(1)} fusion(bf16[8,32,64]{2,1,0:T(8,128)(2,1)S(1)} %pad_maximum_fusion.1, s32[1024]{0:T(1024)S(1)} %pad_clamp_fusion), kind=kCustom, calls=%fused_computation | custom fusion | bytes 65568 | tf_op jit(solution)/shard_map/gather | solution.py:261
  35.9 0.2 convolution_bitcast_fusion
  36.1 0.1 copy.4
  36.2 5.8 %cholesky.16 = f32[64,64]{1,0:T(8,128)S(1)} custom-call(f32[64,64]{1,0:T(8,128)S(1)} %fusion.5), custom_call_target="Cholesky" | custom-call | tf_op jit(solution)/shard_map/jit(cholesky)/cholesky | solution.py:169
  42.1 0.6 %compare_reduce_fusion = pred[]{:T(512)} fusion(f32[64]{0:T(128)S(1)} %select_reduce_fusion), kind=kLoop, calls=%fused_computation.31 | loop fusion | flops 127 | bytes 257 | tf_op jit(solution)/shard_map/jit(cholesky)/cholesky | solution.py:169
  42.7 0.7 %fusion.2 = f32[1,64,64]{2,1,0:T(8,128)S(1)} fusion(f32[64,64]{1,0:T(8,128)S(1)} %cholesky.16, pred[]{:T(512)} %compare_reduce_fusion), kind=kLoop, calls=%fused_computation.16 | loop fusion | flops 16384 | bytes 32769 | tf_op jit(solution)/shard_map/jit(_solve_triangular)/triangular_solve | solution.py:170
  43.4 4.9 %custom-call.7 = f32[1,64,64]{1,2,0:T(8,128)S(1)} custom-call(f32[1,64,64]{2,1,0:T(8,128)S(1)} %fusion.2), custom_call_target="InvertDiagBlocksLowerTriangular" | custom-call | tf_op jit(solution)/shard_map/jit(_solve_triangular)/triangular_solve | solution.py:170
  48.3 0.3 fusion.3
  48.6 0.2 fusion.6
  48.8 0.2 convolution_subtract_fusion.1
  48.9 0.6 %pad_maximum_fusion.3.gain_ref = bf16[128,256]{1,0:T(8,128)(2,1)} fusion(bf16[64,256]{1,0:T(8,128)(2,1)S(1)} %get-tuple-element.5, bf16[64,256]{1,0:T(8,128)(2,1)S(1)} %get-tuple-element.4), kind=kLoop, calls=%fused_computation.14 | loop fusion | flops 131072 | bytes 131072 | tf_op jit(solution)/shard_map/concatenate | solution.py:164
  49.6 0.4 reduce-precision_convert_fusion
  50.0 0.7 %pad_maximum_fusion.keep_ref = bf16[512,256]{1,0:T(8,128)(2,1)} fusion(bf16[256,256]{1,0:T(8,128)(2,1)S(1)} %get-tuple-element.3, bf16[256,256]{1,0:T(8,128)(2,1)S(1)} %get-tuple-element.2), kind=kLoop, calls=%fused_computation.7 | loop fusion | flops 524288 | bytes 524288 | tf_op jit(solution)/shard_map/concatenate | solution.py:164
  50.7 0.0 all-to-all-done.a_ref
  50.7 4.2 %finish.1 = (bf16[16,128,256]{2,1,0:T(8,128)(2,1)}, bf16[64,16,128]{2,1,0:T(8,128)(2,1)}) custom-call(bf16[32,16,1024]{2,1,0:T(8,128)(2,1)S(1)} %all-to-all-done.a_ref, bf16[512,256]{1,0:T(8,128)(2,1)} %pad_maximum_fusion.keep_ref, bf16[128,256]{1,0:T(8,128)(2,1)} %pad_maximum_fusion.3.gain_ref), custom_call_target="tpu_custom_call" | custom-call | tf_op jit(solution)/shard_map/finish/pallas_call | solution.py:142
  (9 shorter events, 0.1 us)
Async XLA Ops:
  3.0 6.9 %collective-permute-start.2 = (bf16[32,64]{1,0:T(8,128)(2,1)}, bf16[32,64]{1,0:T(8,128)(2,1)S(1)}, u32[]{:S(2)}, u32[]{:S(2)}) collective-permute-start(bf16[32,64]{1,0:T(8,128)(2,1)} %pick.1), channel_id=1, source_target_pairs={{0,3},{1,2},{2,1},{3,0},{4,7},{5,6},{6,5},{7,4},{8,11},{9,10},{10,... | collective-permute-start | bytes 12296 | tf_op jit(solution)/shard_map/ppermute | solution.py:159
  8.0 4.8 %collective-permute-start.1 = (bf16[32,64]{1,0:T(8,128)(2,1)}, bf16[32,64]{1,0:T(8,128)(2,1)S(1)}, u32[]{:S(2)}, u32[]{:S(2)}) collective-permute-start(bf16[32,64]{1,0:T(8,128)(2,1)} %pick.1), channel_id=1, source_target_pairs={{0,2},{1,3},{2,0},{3,1},{4,6},{5,7},{6,4},{7,5},{8,10},{9,11},{10,... | collective-permute-start | bytes 12296 | tf_op jit(solution)/shard_map/ppermute | solution.py:159
  8.1 4.8 %collective-permute-start = (bf16[32,64]{1,0:T(8,128)(2,1)}, bf16[32,64]{1,0:T(8,128)(2,1)S(1)}, u32[]{:S(2)}, u32[]{:S(2)}) collective-permute-start(bf16[32,64]{1,0:T(8,128)(2,1)} %pick.1), channel_id=1, source_target_pairs={{0,1},{1,0},{2,3},{3,2},{4,5},{5,4},{6,7},{7,6},{8,9},{9,8},{10,11... | collective-permute-start | bytes 12296 | tf_op jit(solution)/shard_map/ppermute | solution.py:159
  13.5 8.5 %collective-permute-start.3 = (bf16[1,32,64]{2,1,0:T(8,128)(2,1)S(1)}, bf16[1,32,64]{2,1,0:T(8,128)(2,1)S(1)}, u32[]{:S(2)}, u32[]{:S(2)}) collective-permute-start(bf16[1,32,64]{2,1,0:T(8,128)(2,1)S(1)} %add_bitcast_fusion), channel_id=1, source_target_pairs={{0,4},{4,0},{8,12},{12,8},{16,20},{20,16},{24,28},{28,24},{1,5},{5... | collective-permute-start | bytes 12296 | tf_op jit(solution)/shard_map/ppermute | solution.py:159
  17.6 33.1 %all-to-all-start = ((bf16[32,16,1024]{2,1,0:T(8,128)(2,1)}), bf16[32,16,1024]{2,1,0:T(8,128)(2,1)S(1)}, u32[]{:S(2)}, u32[]{:S(2)}) async-start(bf16[32,16,1024]{2,1,0:T(8,128)(2,1)} %bitcast.23), calls=%async_computation | async-start | bytes 2097152 | tf_op jit(solution)/shard_map/all_to_all | solution.py:257
  22.0 8.3 %collective-permute-start.4 = (bf16[2,32,64]{2,1,0:T(8,128)(2,1)S(1)}, bf16[2,32,64]{2,1,0:T(8,128)(2,1)S(1)}, u32[]{:S(2)}, u32[]{:S(2)}) collective-permute-start(bf16[2,32,64]{2,1,0:T(8,128)(2,1)S(1)} %pad_maximum_fusion.6), channel_id=1, source_target_pairs={{0,8},{4,12},{8,0},{12,4},{16,24},{20,28},{24,16},{28,20},{1,9},{5... | collective-permute-start | bytes 24584 | tf_op jit(solution)/shard_map/ppermute | solution.py:159
  30.4 5.0 %collective-permute-start.5 = (bf16[4,32,64]{2,1,0:T(8,128)(2,1)S(1)}, bf16[4,32,64]{2,1,0:T(8,128)(2,1)S(1)}, u32[]{:S(2)}, u32[]{:S(2)}) collective-permute-start(bf16[4,32,64]{2,1,0:T(8,128)(2,1)S(1)} %pad_maximum_fusion.5), channel_id=1, source_target_pairs={{0,16},{4,20},{8,24},{12,28},{16,0},{20,4},{24,8},{28,12},{1,17},{... | collective-permute-start | bytes 49160 | tf_op jit(solution)/shard_map/ppermute | solution.py:159

commit v3 on v2

v3 whole, which is shorter than its diff:
```python
import jax
import jax.numpy as jnp
from jax import lax
from jax.experimental import pallas as pl
from jax.experimental.pallas import tpu as pltpu
from jax.sharding import PartitionSpec as P


highest = lax.Precision.HIGHEST
f32 = jnp.float32
bf16 = jnp.bfloat16
LANES = 128
SUBLANES = 8
AXES = ("pix", "row")


def contract_last(a, b):
    return lax.dot_general(a, b, (((1,), (1,)), ((), ())), preferred_element_type=f32)


def hot(shape, test):
    row = lax.broadcasted_iota(jnp.int32, shape, 0)
    column = lax.broadcasted_iota(jnp.int32, shape, 1)
    return test(row, column).astype(f32).astype(bf16)


def swap_rows(outer, inner):
    size = outer * inner
    return hot((size, size), lambda m, r: r == (m % outer) * inner + m // outer)


def pick(band_images, pivots, row_index):
    band_dev, line_dev, cols = band_images.shape
    panels, panel = pivots.shape
    pivot_count = panels * panel
    shift = cols.bit_length() - 1
    chunks = 4
    step = band_dev // chunks
    rows = step * line_dev

    def kernel(row_ref, x_ref, piv_ref, spec_ref, held_ref, sems):
        def copy(i):
            part = slice(i * step, (i + 1) * step)
            return pltpu.make_async_copy(x_ref.at[part], held_ref.at[part], sems.at[i])

        for i in range(chunks):
            copy(i).start()
        flat = jnp.concatenate([piv_ref[i : i + 1, :] for i in range(panels)], axis=1).astype(f32)
        own = lax.broadcasted_iota(jnp.int32, (pivot_count, pivot_count), 0) == lax.broadcasted_iota(
            jnp.int32, (pivot_count, pivot_count), 1
        )
        flat = jnp.sum(jnp.where(own, flat, 0.0), axis=1, keepdims=True).astype(jnp.int32)
        column = flat & (cols - 1)
        inner = (flat >> shift) - row_ref[0] * line_dev
        chosen = hot((pivot_count, cols), lambda k, c: c == column)
        lane = lax.broadcasted_iota(jnp.int32, (pivot_count, rows), 1)
        inside = lane % line_dev == inner
        fold = hot((step, rows), lambda b, r: r // line_dev == b)
        for i in range(chunks):
            copy(i).wait()
            part = held_ref[i * step : (i + 1) * step].reshape(rows, cols)
            found = jnp.where(inside, contract_last(chosen, part), 0.0).astype(bf16)
            spec_ref[i * step : (i + 1) * step, :] = contract_last(fold, found).astype(bf16)

    return pl.pallas_call(
        kernel,
        out_shape=jax.ShapeDtypeStruct((band_dev, pivot_count), bf16),
        in_specs=[
            pl.BlockSpec(memory_space=pltpu.SMEM),
            pl.BlockSpec(memory_space=pl.ANY),
            pl.BlockSpec(memory_space=pltpu.VMEM),
        ],
        scratch_shapes=[pltpu.VMEM(band_images.shape, bf16), pltpu.SemaphoreType.DMA((chunks,))],
        name="pick",
    )(row_index, band_images, pivots)


def pack(band_images):
    band_dev, line_dev, cols = band_images.shape
    rows = band_dev * line_dev
    taken = LANES // band_dev
    groups = line_dev // taken
    wide = SUBLANES * line_dev
    sides = cols // wide

    def kernel(x_ref, out_ref, held_ref, rows_ref, out_buf, in_sems, out_sems):
        def take(j):
            part = pl.ds(j * wide, wide)
            return pltpu.make_async_copy(x_ref.at[:, :, part], held_ref.at[:, :, part], in_sems.at[j])

        def give(j):
            part = pl.ds(j * wide, wide)
            return pltpu.make_async_copy(out_buf.at[part], out_ref.at[part], out_sems.at[j])

        for j in range(sides):
            take(j).start()
        eye = hot((wide, wide), lambda m, r: m == r)
        mixed = swap_rows(SUBLANES, line_dev)
        for j in range(sides):
            take(j).wait()
            side = slice(j * wide, (j + 1) * wide)
            for i in range(0, band_dev, 2 * SUBLANES):
                low, high = (
                    jnp.dot(
                        mixed,
                        held_ref[k : k + SUBLANES, :, side].reshape(wide, wide),
                        preferred_element_type=f32,
                    )
                    for k in (i, i + SUBLANES)
                )
                for line in range(line_dev):
                    start = ((line % groups) * taken + line // groups) * band_dev + i
                    at = slice(line * SUBLANES, (line + 1) * SUBLANES)
                    rows_ref[start : start + 2 * SUBLANES, side] = jnp.concatenate(
                        [low[at], high[at]], axis=0
                    ).astype(bf16)
            out_buf[side, :] = contract_last(eye, rows_ref[:, side]).astype(bf16)
            give(j).start()
        for j in range(sides):
            give(j).wait()

    return pl.pallas_call(
        kernel,
        out_shape=jax.ShapeDtypeStruct((cols, rows), bf16),
        in_specs=[pl.BlockSpec(memory_space=pl.ANY)],
        out_specs=pl.BlockSpec(memory_space=pl.ANY),
        scratch_shapes=[
            pltpu.VMEM(band_images.shape, bf16),
            pltpu.VMEM((rows, cols), bf16),
            pltpu.VMEM((cols, rows), bf16),
            pltpu.SemaphoreType.DMA((sides,)),
            pltpu.SemaphoreType.DMA((sides,)),
        ],
        name="pack",
    )(band_images)


def finish(arrived, keep, gains, pix_count, row_count, band_dev, line_dev):
    _, narrow, _ = arrived.shape
    taken = LANES // band_dev
    groups = line_dev // taken
    lines = row_count * line_dev
    bands = pix_count * band_dev
    kept = gains.shape[0] // 2
    width = 4
    joined = bands // LANES
    pieces = narrow // width

    def swap(low, high, shift, mask):
        return (
            jnp.where(mask, low, pltpu.roll(high, shift, 1)),
            jnp.where(mask, pltpu.roll(low, LANES - shift, 1), high),
        )

    def kernel(a_ref, keep_ref, gain_ref, res_ref, coef_ref, x_ref, hold_ref, res_buf, coef_buf, sems):
        def give(i):
            part = pl.ds(i * width, width)
            return pltpu.make_async_copy(res_buf.at[part], res_ref.at[part], sems.at[i])

        last = pltpu.make_async_copy(coef_buf, coef_ref, sems.at[pieces])
        lane = lax.broadcasted_iota(jnp.int32, (SUBLANES, LANES), 1)
        half = groups * narrow
        mixed = hot(
            (2 * half, 2 * half),
            lambda m, r: r == (m // half) * half + (m % groups) * narrow + (m % half) // groups,
        )
        for r in range(row_count):
            for j in range(joined):
                sides = []
                for n in range(taken // 2):
                    tall = []
                    for s in range(2):
                        source = (j * taken + s * (taken // 2) + n) * row_count + r
                        tall += [a_ref[source, :, g * LANES : (g + 1) * LANES] for g in range(groups)]
                    sides.append(jnp.concatenate(tall, axis=0))
                turned = jnp.dot(mixed, jnp.concatenate(sides, axis=1), preferred_element_type=f32)
                for c in range(narrow):
                    v = []
                    for i in range(taken):
                        s, n = i // (taken // 2), i % (taken // 2)
                        start = (s * narrow + c) * groups
                        v.append(turned[start : start + groups, n * LANES : (n + 1) * LANES])
                    step = taken // 2
                    while step >= 1:
                        shift = step * band_dev
                        mask = (lane // shift) % 2 == 0
                        w = list(v)
                        for i in range(taken):
                            if (i // step) % 2 == 0:
                                w[i], w[i + step] = swap(v[i], v[i + step], shift, mask)
                        v = w
                        step //= 2
                    row = c * lines + r * line_dev
                    x_ref[row : row + line_dev, j * LANES : (j + 1) * LANES] = (
                        jnp.concatenate(v, axis=0).astype(bf16)
                    )
        for c in range(0, narrow, 2):
            found = contract_last(gain_ref[...], x_ref[c * lines : (c + 2) * lines, :])
            found = (found[:kept] + found[kept:]).astype(bf16)
            hold_ref[c] = found[:, :lines]
            hold_ref[c + 1] = found[:, lines:]
        turn = swap_rows(narrow, narrow)
        for k in range(0, kept, 2 * narrow):
            tall = [
                jnp.concatenate([hold_ref[c, q : q + narrow, :] for c in range(narrow)], axis=0)
                for q in (k, k + narrow)
            ]
            turned = jnp.dot(turn, jnp.concatenate(tall, axis=1), preferred_element_type=f32).astype(bf16)
            coef_buf[k : k + narrow] = turned[:, :lines].reshape(narrow, narrow, lines)
            coef_buf[k + narrow : k + 2 * narrow] = turned[:, lines:].reshape(narrow, narrow, lines)
        last.start()
        for p in range(pieces):
            pixels = x_ref[p * width * lines : (p + 1) * width * lines, :]
            both = jnp.dot(pixels, keep_ref[:bands], preferred_element_type=f32)
            both = both + jnp.dot(pixels, keep_ref[bands:], preferred_element_type=f32)
            res_buf[p * width : (p + 1) * width] = both.astype(bf16).reshape(width, lines, bands)
            give(p).start()
        last.wait()
        for p in range(pieces):
            give(p).wait()

    near = [pltpu.with_memory_space_constraint(v, pltpu.VMEM) for v in (arrived, keep, gains)]
    return pl.pallas_call(
        kernel,
        out_shape=(
            jax.ShapeDtypeStruct((narrow, lines, bands), bf16),
            jax.ShapeDtypeStruct((kept, narrow, lines), bf16),
        ),
        out_specs=(pl.BlockSpec(memory_space=pl.ANY), pl.BlockSpec(memory_space=pl.ANY)),
        scratch_shapes=[
            pltpu.VMEM((narrow * lines, bands), bf16),
            pltpu.VMEM((narrow, kept, lines), bf16),
            pltpu.VMEM((narrow, lines, bands), bf16),
            pltpu.VMEM((kept, narrow, lines), bf16),
            pltpu.SemaphoreType.DMA((pieces + 1,)),
        ],
        name="finish",
    )(*near)


def factor(spectra):
    bands, count = spectra.shape
    half = count // 2

    def kernel(s_ref, keep_ref, gain_ref):
        s = s_ref[...].astype(f32)
        st = s.T
        gram = jnp.dot(st, s, precision=highest, preferred_element_type=f32)
        row = lax.broadcasted_iota(jnp.int32, (count, 2 * count), 0)
        lane = lax.broadcasted_iota(jnp.int32, (count, 2 * count), 1)
        both = jnp.concatenate([gram, jnp.where(lane == row, 1.0, 0.0)[:, :count]], axis=1)
        done = []
        for j in range(count):
            base = j // SUBLANES * SUBLANES
            scale = 1.0 / jnp.sqrt(both[j - base : j - base + 1, j : j + 1])
            top = both[j - base : j - base + 1, :] * scale
            done.append(top[:, count:])
            if (j + 1) % SUBLANES == 0:
                both = both[SUBLANES:]
            if j + 1 < count:
                column = both[:, j : j + 1] * scale
                both = both - column * top
        inverse = jnp.concatenate(done, axis=0)
        basis = jnp.dot(inverse, st, precision=highest, preferred_element_type=f32)
        tall = basis.T
        cross = lax.dot_general(
            basis[:half], basis[half:], (((1,), (1,)), ((), ())), precision=highest, preferred_element_type=f32
        )
        second = tall[:, half:] - jnp.dot(tall[:, :half], cross, precision=highest, preferred_element_type=f32)
        gains = jnp.concatenate([tall[:, :half], second], axis=1)
        keep = jnp.where(
            lax.broadcasted_iota(jnp.int32, (bands, bands), 0)
            == lax.broadcasted_iota(jnp.int32, (bands, bands), 1),
            1.0,
            0.0,
        ) - jnp.dot(gains, basis, precision=highest, preferred_element_type=f32)
        gains = gains.T
        for ref, value, size in ((keep_ref, keep, bands), (gain_ref, gains, count)):
            high = value.astype(bf16)
            ref[:size] = high
            ref[size:] = (value - high.astype(f32)).astype(bf16)

    return pl.pallas_call(
        kernel,
        out_shape=(
            pltpu.VMEM((2 * bands, bands), bf16),
            pltpu.VMEM((2 * count, bands), bf16),
        ),
        name="factor",
    )(spectra)


def exchange(x, axis, k):
    count = lax.axis_size(axis)
    return lax.ppermute(x, axis, [(i, i ^ k) for i in range(count)])


def orthonormal(spectra):
    gram = jnp.dot(spectra, spectra.T, precision=highest)
    factor = jnp.linalg.cholesky(gram)
    return jax.scipy.linalg.solve_triangular(factor, spectra, lower=True)


def project(block, basis):
    count = basis.shape[0] // 2
    first = basis[:count]
    second = basis[count:]
    coef_one = jnp.einsum("clb,kb->kcl", block, first, precision=highest)
    remain = block - jnp.einsum("kcl,kb->clb", coef_one, first, precision=highest)
    coef_two = jnp.einsum("clb,kb->kcl", remain, second, precision=highest)
    remain = remain - jnp.einsum("kcl,kb->clb", coef_two, second, precision=highest)
    return (
        remain.astype(bf16),
        jnp.concatenate([coef_one, coef_two], axis=0).astype(bf16),
    )


def plain(band_images, line_index, column, pix_count, row_count, narrow):
    band_dev, line_dev, cols_all = band_images.shape
    offset = line_index - lax.axis_index("row") * line_dev
    inside = (offset >= 0) & (offset < line_dev)
    position = jnp.clip(offset, 0, line_dev - 1) * cols_all + column
    picked = jnp.take(band_images.reshape(band_dev, line_dev * cols_all), position, axis=1)
    picked = jnp.where(inside[None, :], picked, jnp.zeros_like(picked))
    stacked = lax.all_gather(picked, "pix", axis=0, tiled=True)
    spectra = lax.psum(stacked.astype(f32).astype(bf16), "row").astype(f32)
    basis = orthonormal(spectra.T)
    shaped = band_images.reshape(band_dev, line_dev, pix_count, row_count, narrow)
    arrived = lax.all_to_all(
        lax.all_to_all(shaped, "pix", split_axis=2, concat_axis=0, tiled=True),
        "row",
        split_axis=3,
        concat_axis=1,
        tiled=True,
    )
    block = (
        arrived.reshape(arrived.shape[0], arrived.shape[1], narrow)
        .transpose(2, 1, 0)
        .astype(f32)
    )
    return project(block, basis)


def shards(band_images, pivots):
    band_dev, line_dev, cols_all = band_images.shape
    pix_count = lax.axis_size("pix")
    row_count = lax.axis_size("row")
    part_count = pix_count * row_count
    narrow = cols_all // part_count
    flat_pivots = pivots.reshape(-1)
    pivot_count = flat_pivots.shape[0]
    line_index = flat_pivots // cols_all
    column = flat_pivots % cols_all
    lines = row_count * line_dev
    bands = pix_count * band_dev
    taken = LANES // band_dev
    fits = (
        taken * band_dev == LANES
        and taken in (2, 4)
        and line_dev == SUBLANES * taken
        and narrow == 16
        and cols_all % (SUBLANES * line_dev) == 0
        and lines == LANES
        and 2 * pivot_count == LANES
        and bands % LANES == 0
        and cols_all & (cols_all - 1) == 0
        and pix_count & (pix_count - 1) == 0
        and row_count & (row_count - 1) == 0
    )
    if not fits:
        return plain(band_images, line_index, column, pix_count, row_count, narrow)
    row_index = lax.axis_index("row").astype(jnp.int32).reshape(1)
    picked = pick(band_images, pivots, row_index)
    found = picked
    for k in range(1, row_count):
        found = found + exchange(picked, "row", k)
    packed = pack(band_images).reshape(part_count, narrow, line_dev * band_dev)
    arrived = lax.all_to_all(packed, AXES, 0, 0, tiled=True)
    for k in range(pix_count.bit_length() - 1):
        other = exchange(found, "pix", 1 << k)
        after = (lax.axis_index("pix") >> k) % 2 == 1
        found = jnp.where(after, jnp.concatenate([other, found], axis=0), jnp.concatenate([found, other], axis=0))
    keep, gains = factor(found)
    return finish(arrived, keep, gains, pix_count, row_count, band_dev, line_dev)


def solution(mesh):
    placed = (P("pix", "row", None), P())
    return jax.shard_map(
        shards,
        mesh=mesh,
        in_specs=placed,
        out_specs=(P(AXES, None, None), P(None, AXES, None)),
        check_vma=False,
    )
```

time: 55.2 us -> 59.8 us (1.083)
  other arithmetic: 14.2 us -> 1.37 us
  waiting for transfers between devices: 14.1 us -> 24.5 us
  Pallas kernels: 10.6 us -> 18 us
  starting transfers between devices: 13.4 us -> 14.9 us
  matrix products: 1.18 us -> 0 us
  local copies, waits for them, and re-layouts: 0.64 us -> 0 us
    another operation x6 -> x0, other arithmetic: 12.1 us -> none  [the longest x3 6.52 us: orthonormal(): factor = jnp.linalg.cholesky(gram)]
    ppermute x6, waiting for transfers between devices: 14.1 us -> 24.5 us  [exchange(): return lax.ppermute(x, axis, [(i, i ^ k) for i in range(count)])]
    pallas_call x0 -> x1, Pallas kernels: none -> 8.4 us  [factor(): pl.pallas_call(kernel, out_shape=(pltpu.VMEM((2 * bands, bands), bf16), p...]
    all_to_all x1, starting transfers between devices: 4.39 us -> 7.33 us  [shards(): arrived = lax.all_to_all(packed, AXES, 0, 0, tiled=True)]
    pallas_call x1, Pallas kernels: 2.34 us -> 3.81 us  [pick(): pl.pallas_call(kernel, out_shape=jax.ShapeDtypeStruct((band_dev, pivot_co...]
    ppermute x6, starting transfers between devices: 9 us -> 7.54 us  [exchange(): return lax.ppermute(x, axis, [(i, i ^ k) for i in range(count)])]
    pallas_call x1, Pallas kernels: 4.19 us -> 2.75 us  [finish(): pl.pallas_call(kernel, out_shape=(jax.ShapeDtypeStruct((narrow, lines, ba...]
    concatenate x5 -> x0, other arithmetic: 1.37 us -> none  [the longest x2 1.33 us: split(): return jnp.concatenate([high, a - high], axis=0).astype(bf16)]
  transfers between devices with their start and end apart: 7 -> 7, of which waited for: 4 -> 5; matrix products, arithmetic and copies ran while one was open for 28% -> 2% of each run, Pallas kernels for 7% -> 21%
where the time goes in v3:
time: 59.8 us; the launch traced here: 59.5 us
  waiting for transfers between devices  24.5 us (41%)
  Pallas kernels  18 us (30%)
  starting transfers between devices  14.9 us (25%)
  other arithmetic  1.37 us (2%)
  between operations  0.69 us (1%)
    ppermute x6, waiting for transfers between devices, exchange(): return lax.ppermute(x, axis, [(i, i ^ k) for i in range(count)])  24.5 us
    pallas_call x1, Pallas kernels, factor(): pl.pallas_call(kernel, out_shape=(pltpu.VMEM((2 * bands, bands), bf16), p...  8.4 us
    ppermute x6, starting transfers between devices, exchange(): return lax.ppermute(x, axis, [(i, i ^ k) for i in range(count)])  7.54 us
    all_to_all x1, starting transfers between devices, shards(): arrived = lax.all_to_all(packed, AXES, 0, 0, tiled=True)  7.33 us
    pallas_call x1, Pallas kernels, pick(): pl.pallas_call(kernel, out_shape=jax.ShapeDtypeStruct((band_dev, pivot_co...  3.81 us
    pallas_call x1, Pallas kernels, pack(): pl.pallas_call(kernel, out_shape=jax.ShapeDtypeStruct((cols, rows), bf16)...  3.07 us
    pallas_call x1, Pallas kernels, finish(): pl.pallas_call(kernel, out_shape=(jax.ShapeDtypeStruct((narrow, lines, ba...  2.75 us
  transfers between devices with their start and end apart: 7, of which 5 were waited for; matrix products, arithmetic and copies ran while one was open for 2% of the time, Pallas kernels for 21%

profile of v3, /device:TPU:0, one launch (start us, length us, event | category | flops | bytes accessed | tf_op | source)
XLA Modules:
  0.0 59.5 jit_solution(15540545118278423655)
XLA Ops:
  0.6 3.1 %pack.1 = bf16[512,1024]{1,0:T(8,128)(2,1)} custom-call(bf16[32,32,512]{2,1,0:T(8,128)(2,1)} %x_ref.3), custom_call_target="tpu_custom_call" | custom-call | tf_op jit(solution)/shard_map/pack/pallas_call | solution.py:122
  3.7 7.3 %all-to-all-start = ((bf16[32,16,1024]{2,1,0:T(8,128)(2,1)}), bf16[32,16,1024]{2,1,0:T(8,128)(2,1)S(1)}, u32[]{:S(2)}, u32[]{:S(2)}) async-start(bf16[32,16,1024]{2,1,0:T(8,128)(2,1)} %bitcast.2), calls=%async_computation | async-start | bytes 2097152 | tf_op jit(solution)/shard_map/all_to_all | solution.py:378
  11.0 3.8 %pick.1 = bf16[32,64]{1,0:T(8,128)(2,1)} custom-call(s32[1]{0:T(128)} %bitcast.1.row_ref, bf16[32,32,512]{2,1,0:T(8,128)(2,1)} %x_ref.3, s32[2,32]{1,0:T(2,128)} %piv_ref.1), custom_call_target="tpu_custom_call" | custom-call | tf_op jit(solution)/shard_map/pick/pallas_call | solution.py:65
  14.9 3.7 %collective-permute-start.2 = (bf16[32,64]{1,0:T(8,128)(2,1)}, bf16[32,64]{1,0:T(8,128)(2,1)S(1)}, u32[]{:S(2)}, u32[]{:S(2)}) collective-permute-start(bf16[32,64]{1,0:T(8,128)(2,1)} %pick.1), channel_id=1, source_target_pairs={{0,3},{1,2},{2,1},{3,0},{4,7},{5,6},{6,5},{7,4},{8,11},{9,10},{10,... | collective-permute-start | bytes 12296 | tf_op jit(solution)/shard_map/ppermute | solution.py:295
  18.5 0.0 collective-permute-start.1
  18.5 0.8 %collective-permute-start = (bf16[32,64]{1,0:T(8,128)(2,1)}, bf16[32,64]{1,0:T(8,128)(2,1)S(1)}, u32[]{:S(2)}, u32[]{:S(2)}) collective-permute-start(bf16[32,64]{1,0:T(8,128)(2,1)} %pick.1), channel_id=1, source_target_pairs={{0,1},{1,0},{2,3},{3,2},{4,5},{5,4},{6,7},{7,6},{8,9},{9,8},{10,11... | collective-permute-start | bytes 12296 | tf_op jit(solution)/shard_map/ppermute | solution.py:295
  19.3 13.6 %collective-permute-done.2 = bf16[32,64]{1,0:T(8,128)(2,1)S(1)} collective-permute-done((bf16[32,64]{1,0:T(8,128)(2,1)}, bf16[32,64]{1,0:T(8,128)(2,1)S(1)}, u32[]{:S(2)}, u32[]{:S(2)}) %collective-permute-start.2) | collective-permute-done | bytes 4128 | tf_op jit(solution)/shard_map/ppermute | solution.py:295
  32.9 5.0 %collective-permute-done.1 = bf16[32,64]{1,0:T(8,128)(2,1)S(1)} collective-permute-done((bf16[32,64]{1,0:T(8,128)(2,1)}, bf16[32,64]{1,0:T(8,128)(2,1)S(1)}, u32[]{:S(2)}, u32[]{:S(2)}) %collective-permute-start.1) | collective-permute-done | bytes 4128 | tf_op jit(solution)/shard_map/ppermute | solution.py:295
  37.9 0.0 collective-permute-done
  37.9 0.7 %add_add_fusion = bf16[32,64]{1,0:T(8,128)(2,1)S(1)} fusion(bf16[32,64]{1,0:T(8,128)(2,1)S(1)} %collective-permute-done.2, bf16[32,64]{1,0:T(8,128)(2,1)S(1)} %collective-permute-done.1, bf16[32,64]{1,0:T(8,128)(2,1)} %pick.1, bf16[32,64]{1,0:T(8,128)(2,1)S(1)} %collective-permute-done), kind=kLoop, calls=%fused_computation.3 | loop fusion | flops 6144 | bytes 20480 | tf_op jit(solution)/shard_map/add | solution.py:376
  38.7 0.0 collective-permute-start.3
  38.7 1.2 %collective-permute-done.3 = bf16[32,64]{1,0:T(8,128)(2,1)S(1)} collective-permute-done((bf16[32,64]{1,0:T(8,128)(2,1)S(1)}, bf16[32,64]{1,0:T(8,128)(2,1)S(1)}, u32[]{:S(2)}, u32[]{:S(2)}) %collective-permute-start.3) | collective-permute-done | bytes 4128 | tf_op jit(solution)/shard_map/ppermute | solution.py:295
  39.8 1.5 %collective-permute-start.4 = (bf16[64,64]{1,0:T(8,128)(2,1)S(1)}, bf16[64,64]{1,0:T(8,128)(2,1)S(1)}, u32[]{:S(2)}, u32[]{:S(2)}) collective-permute-start(bf16[64,64]{1,0:T(8,128)(2,1)S(1)} %maximum_select_fusion.2), channel_id=1, source_target_pairs={{0,8},{4,12},{8,0},{12,4},{16,24},{20,28},{24,16},{28,20},{1,9},{5... | collective-permute-start | bytes 24584 | tf_op jit(solution)/shard_map/ppermute | solution.py:295
  41.4 2.3 %collective-permute-done.4 = bf16[64,64]{1,0:T(8,128)(2,1)S(1)} collective-permute-done((bf16[64,64]{1,0:T(8,128)(2,1)S(1)}, bf16[64,64]{1,0:T(8,128)(2,1)S(1)}, u32[]{:S(2)}, u32[]{:S(2)}) %collective-permute-start.4) | collective-permute-done | bytes 8224 | tf_op jit(solution)/shard_map/ppermute | solution.py:295
  43.7 1.5 %collective-permute-start.5 = (bf16[128,64]{1,0:T(8,128)(2,1)S(1)}, bf16[128,64]{1,0:T(8,128)(2,1)S(1)}, u32[]{:S(2)}, u32[]{:S(2)}) collective-permute-start(bf16[128,64]{1,0:T(8,128)(2,1)S(1)} %maximum_select_fusion.1), channel_id=1, source_target_pairs={{0,16},{4,20},{8,24},{12,28},{16,0},{20,4},{24,8},{28,12},{1,17},{... | collective-permute-start | bytes 49160 | tf_op jit(solution)/shard_map/ppermute | solution.py:295
  45.2 2.4 %collective-permute-done.5 = bf16[128,64]{1,0:T(8,128)(2,1)S(1)} collective-permute-done((bf16[128,64]{1,0:T(8,128)(2,1)S(1)}, bf16[128,64]{1,0:T(8,128)(2,1)S(1)}, u32[]{:S(2)}, u32[]{:S(2)}) %collective-permute-start.5) | collective-permute-done | bytes 16416 | tf_op jit(solution)/shard_map/ppermute | solution.py:295
  47.6 0.7 %maximum_select_fusion.s_ref = bf16[256,64]{1,0:T(8,128)(2,1)} fusion(bf16[128,64]{1,0:T(8,128)(2,1)S(1)} %maximum_select_fusion.1, bf16[128,64]{1,0:T(8,128)(2,1)S(1)} %collective-permute-done.5, pred[]{:T(512)S(6)} %eq.13), kind=kLoop, calls=%fused_computation | loop fusion | flops 147456 | bytes 65537 | tf_op jit(solution)/shard_map/jit(_where)/select_n | solution.py:382
  48.3 8.4 %factor.1 = (bf16[512,256]{1,0:T(8,128)(2,1)S(1)}, bf16[128,256]{1,0:T(8,128)(2,1)S(1)}) custom-call(bf16[256,64]{1,0:T(8,128)(2,1)} %maximum_select_fusion.s_ref), custom_call_target="tpu_custom_call" | custom-call | tf_op jit(solution)/shard_map/factor/pallas_call | solution.py:283
  56.7 0.0 all-to-all-done.a_ref
  56.7 2.7 %finish.1 = (bf16[16,128,256]{2,1,0:T(8,128)(2,1)}, bf16[64,16,128]{2,1,0:T(8,128)(2,1)}) custom-call(bf16[32,16,1024]{2,1,0:T(8,128)(2,1)S(1)} %all-to-all-done.a_ref, bf16[512,256]{1,0:T(8,128)(2,1)S(1)} %get-tuple-element.4.keep_ref, bf16[128,256]{1,0:T(8,128)(2,1)S(1)} %get-tuple-element.5.gain_ref), custom_call_target="tpu_custom_call" | custom-call | tf_op jit(solution)/shard_map/finish/pallas_call | solution.py:223
  (2 shorter events, 0.0 us)
Async XLA Ops:
  3.7 53.0 %all-to-all-start = ((bf16[32,16,1024]{2,1,0:T(8,128)(2,1)}), bf16[32,16,1024]{2,1,0:T(8,128)(2,1)S(1)}, u32[]{:S(2)}, u32[]{:S(2)}) async-start(bf16[32,16,1024]{2,1,0:T(8,128)(2,1)} %bitcast.2), calls=%async_computation | async-start | bytes 2097152 | tf_op jit(solution)/shard_map/all_to_all | solution.py:378
  14.9 18.1 %collective-permute-start.2 = (bf16[32,64]{1,0:T(8,128)(2,1)}, bf16[32,64]{1,0:T(8,128)(2,1)S(1)}, u32[]{:S(2)}, u32[]{:S(2)}) collective-permute-start(bf16[32,64]{1,0:T(8,128)(2,1)} %pick.1), channel_id=1, source_target_pairs={{0,3},{1,2},{2,1},{3,0},{4,7},{5,6},{6,5},{7,4},{8,11},{9,10},{10,... | collective-permute-start | bytes 12296 | tf_op jit(solution)/shard_map/ppermute | solution.py:295
  18.5 19.4 %collective-permute-start.1 = (bf16[32,64]{1,0:T(8,128)(2,1)}, bf16[32,64]{1,0:T(8,128)(2,1)S(1)}, u32[]{:S(2)}, u32[]{:S(2)}) collective-permute-start(bf16[32,64]{1,0:T(8,128)(2,1)} %pick.1), channel_id=1, source_target_pairs={{0,2},{1,3},{2,0},{3,1},{4,6},{5,7},{6,4},{7,5},{8,10},{9,11},{10,... | collective-permute-start | bytes 12296 | tf_op jit(solution)/shard_map/ppermute | solution.py:295
  18.5 19.4 %collective-permute-start = (bf16[32,64]{1,0:T(8,128)(2,1)}, bf16[32,64]{1,0:T(8,128)(2,1)S(1)}, u32[]{:S(2)}, u32[]{:S(2)}) collective-permute-start(bf16[32,64]{1,0:T(8,128)(2,1)} %pick.1), channel_id=1, source_target_pairs={{0,1},{1,0},{2,3},{3,2},{4,5},{5,4},{6,7},{7,6},{8,9},{9,8},{10,11... | collective-permute-start | bytes 12296 | tf_op jit(solution)/shard_map/ppermute | solution.py:295
  38.7 1.2 %collective-permute-start.3 = (bf16[32,64]{1,0:T(8,128)(2,1)S(1)}, bf16[32,64]{1,0:T(8,128)(2,1)S(1)}, u32[]{:S(2)}, u32[]{:S(2)}) collective-permute-start(bf16[32,64]{1,0:T(8,128)(2,1)S(1)} %add_add_fusion), channel_id=1, source_target_pairs={{0,4},{4,0},{8,12},{12,8},{16,20},{20,16},{24,28},{28,24},{1,5},{5... | collective-permute-start | bytes 12296 | tf_op jit(solution)/shard_map/ppermute | solution.py:295
  39.8 3.8 %collective-permute-start.4 = (bf16[64,64]{1,0:T(8,128)(2,1)S(1)}, bf16[64,64]{1,0:T(8,128)(2,1)S(1)}, u32[]{:S(2)}, u32[]{:S(2)}) collective-permute-start(bf16[64,64]{1,0:T(8,128)(2,1)S(1)} %maximum_select_fusion.2), channel_id=1, source_target_pairs={{0,8},{4,12},{8,0},{12,4},{16,24},{20,28},{24,16},{28,20},{1,9},{5... | collective-permute-start | bytes 24584 | tf_op jit(solution)/shard_map/ppermute | solution.py:295
  43.7 4.0 %collective-permute-start.5 = (bf16[128,64]{1,0:T(8,128)(2,1)S(1)}, bf16[128,64]{1,0:T(8,128)(2,1)S(1)}, u32[]{:S(2)}, u32[]{:S(2)}) collective-permute-start(bf16[128,64]{1,0:T(8,128)(2,1)S(1)} %maximum_select_fusion.1), channel_id=1, source_target_pairs={{0,16},{4,20},{8,24},{12,28},{16,0},{20,4},{24,8},{28,12},{1,17},{... | collective-permute-start | bytes 49160 | tf_op jit(solution)/shard_map/ppermute | solution.py:295
